TPU v7x, 16 devices: a whole 2x2x2 slice. The times are simulated.
16 devices in a mesh: dp: 2 (over z), sp: 8 (over y, x, core).
Axes of the slice: x: 2, y: 2, z: 2, core: 2. Of those that a mesh axis runs over, the one named last changes fastest.
Arguments:
- x: bfloat16 [16, 2048], P('dp'), parts along dimension 0
- lens: int32 [16], P('dp'), parts along dimension 0
- wq: bfloat16 [2, 2048, 2048], replicated
- wk: bfloat16 [2, 2048, 512], replicated
- wv: bfloat16 [2, 2048, 512], replicated
- wo: bfloat16 [2, 2048, 2048], P(None, 'sp')
- w1: bfloat16 [2, 2048, 8192], P(None, None, 'sp')
- w2: bfloat16 [2, 8192, 2048], P(None, 'sp')
- g1: bfloat16 [2, 2048], replicated
- g2: bfloat16 [2, 2048], replicated
- kc: bfloat16 [2, 16, 4096, 8, 64], P(None, 'dp', 'sp'), parts along dimension 1
- vc: bfloat16 [2, 16, 4096, 8, 64], P(None, 'dp', 'sp'), parts along dimension 1
Outputs:
- output 1: bfloat16 [16, 2048], P('dp'), parts along dimension 0
- output 2: bfloat16 [2, 16, 4096, 8, 64], P(None, 'dp', 'sp'), parts along dimension 1
- output 3: bfloat16 [2, 16, 4096, 8, 64], P(None, 'dp', 'sp'), parts along dimension 1
There are 2 independent parts. A program takes and returns all parts, laid end to end along the dimension named above; an argument that names none is the same for every part.
All inputs are finite; a program needn't handle non-finite values.
Results may differ from a plain program's by a relative error of at most 0.00905547.
Values are sent between devices in bfloat16 or wider.
A program may use at most 1 GiB of HBM per device.

v0:
```python
import jax
import jax.numpy as jnp
from jax import lax
from jax.sharding import PartitionSpec as P

EPS = 1e-6


def _rms(h, g):
    r = lax.rsqrt(jnp.mean(h * h, axis=-1, keepdims=True) + EPS)
    return (h * r * g.astype(jnp.float32)).astype(jnp.bfloat16)


def _mm(a, w):
    return jnp.dot(a, w, preferred_element_type=jnp.float32)


def solution(mesh):
    sp = mesh.shape['sp']
    kspec = P(None, 'dp', 'sp', None, None)

    def local(x, lens, wq, wk, wv, wo, w1, w2, g1, g2, kc, vc):
        nl, b, s_dev, kvh, dh = kc.shape
        hq = wq.shape[-1] // dh
        grp = hq // kvh
        hl = hq // sp
        idx = lax.axis_index('sp')
        posn = idx * s_dev + jnp.arange(s_dev)
        write = (posn[None, :] == (lens - 1)[:, None])[:, :, None, None]
        valid = (posn[None, :] < lens[:, None])[:, None, None, :]
        h = x.astype(jnp.float32)
        ks, vs = [], []
        for l in range(nl):
            xn = _rms(h, g1[l])
            q = _mm(xn, wq[l]).astype(jnp.bfloat16).reshape(b, kvh, grp, dh)
            k = _mm(xn, wk[l]).astype(jnp.bfloat16).reshape(b, 1, kvh, dh)
            v = _mm(xn, wv[l]).astype(jnp.bfloat16).reshape(b, 1, kvh, dh)
            kl = jnp.where(write, k, kc[l])
            vl = jnp.where(write, v, vc[l])
            ks.append(kl)
            vs.append(vl)
            s = jnp.einsum('bkgd,bskd->bkgs', q, kl, preferred_element_type=jnp.float32) * dh ** -0.5
            s = jnp.where(valid, s, -jnp.inf)
            m = jnp.max(s, axis=-1)
            p = jnp.exp(s - jnp.where(jnp.isfinite(m), m, 0.0)[..., None])
            den = jnp.sum(p, axis=-1)
            o = jnp.einsum('bkgs,bskd->bkgd', p.astype(jnp.bfloat16), vl, preferred_element_type=jnp.float32)
            c = jnp.exp(m - lax.pmax(m, 'sp'))
            o, den = lax.psum((o * c[..., None], den * c), 'sp')
            att = (o / den[..., None]).astype(jnp.bfloat16).reshape(b, hq, dh)
            att = lax.dynamic_slice_in_dim(att, idx * hl, hl, axis=1).reshape(b, hl * dh)
            h = h + lax.psum(_mm(att, wo[l]), 'sp')
            u = jax.nn.gelu(_mm(_rms(h, g2[l]), w1[l])).astype(jnp.bfloat16)
            h = h + lax.psum(_mm(u, w2[l]), 'sp')
        return h.astype(jnp.bfloat16), jnp.stack(ks), jnp.stack(vs)

    return jax.shard_map(
        local, mesh=mesh,
        in_specs=(P('dp', None), P('dp'), P(), P(), P(), P(None, 'sp', None), P(None, None, 'sp'),
                  P(None, 'sp', None), P(), P(), kspec, kspec),
        out_specs=(P('dp', None), kspec, kspec), check_vma=False)
```

profile of v0, /device:TPU:0, one launch (start us, length us, event | category | flops | bytes accessed | tf_op | source)
XLA Modules:
  0.0 390.8 jit_solution(12780771400837554702)
XLA Ops:
  7.2 0.7 broadcast_add_fusion
  7.9 0.9 fusion.84
  8.8 0.8 slice_convert_fusion.1
  9.6 2.0 fusion.58
  11.6 0.1 broadcast_in_dim.101
  11.7 4.6 %fusion.30 = bf16[8,2048]{1,0:T(8,128)(2,1)S(1)} fusion(bf16[2,2048,2048]{2,1,0:T(8,128)(2,1)} %param.14, bf16[8,2048]{1,0:T(8,128)(2,1)} %param.12, f32[2048]{0:T(1024)S(1)} %bitcast.102, f32[8]{0:T(128)S(1)} %add_rsqrt_fusion.3), kind=kOutput, calls=%fused_computation.40 | convolution fusion | flops 67190784 | bytes 8462368 | tf_op jit(solution)/shard_map/dot_general | solution.py:15
  16.3 0.1 reshape.131
  16.5 0.1 broadcast_compare_fusion.1
  16.6 3.0 fusion.146
  19.6 25.8 %pmax.14 = f32[8,8,4]{2,1,0:T(8,128)S(1)} all-reduce(f32[8,8,4]{2,1,0:T(8,128)S(1)} %get-tuple-element.23), channel_id=1, replica_groups=mesh['dp'=2,'sp'=8] {'sp'}, use_global_device_ids=true, to_apply=%region_2.3 | all-reduce | flops 256 | bytes 2048 | tf_op jit(solution)/shard_map/pmax | solution.py:48
  45.4 2.0 fusion.61
  47.4 0.1 broadcast_in_dim.105
  47.5 0.4 fusion.76
  47.9 4.3 %fusion.54 = f32[8,8,4,64]{3,2,1,0:T(4,128)} fusion(pred[8,512]{1,0:T(8,128)(4,1)S(1)} %get-tuple-element.22, bf16[2,8,512,8,64]{2,4,3,1,0:T(8,128)(2,1)} %param.23, bf16[8,8,64]{2,1,0:T(8,128)(2,1)S(1)} %broadcast_in_dim.105, f32[8,8,4,512]{3,2,1,0:T(4,128)S(1)} %get-tuple-element.24, f32[8,8,4]{2,1,0:T(8,128)S(1)} %is-finite_select_fusion.1, ...), kind=kOutput, calls=%fused_computation.60 | convolution fusion | flops 19152896 | bytes 4798464 | tf_op jit(solution)/shard_map/bkgs,bskd->bkgd/dot_general | solution.py:47
  52.3 22.3 %psum.57 = f32[8,8,4]{2,1,0:T(8,128)S(1)} all-reduce(f32[8,8,4]{2,1,0:T(8,128)S(1)} %get-tuple-element.9), channel_id=1, replica_groups=mesh['dp'=2,'sp'=8] {'sp'}, use_global_device_ids=true, to_apply=%region_5.6 | all-reduce | flops 256 | bytes 2048 | tf_op jit(solution)/shard_map/psum | solution.py:49
  74.6 22.7 %all-reduce.7.cloned.1.call-done = f32[8,8,4,64]{3,2,1,0:T(4,128)} async-done(((f32[8,8,4,64]{3,2,1,0:T(4,128)}), f32[8,8,4,64]{3,2,1,0:T(4,128)}) %all-reduce.7.cloned.1.call-update) | async-done | bytes 65552 | tf_op jit(solution)/shard_map/psum | solution.py:49
  97.3 1.0 divide_convert_fusion.1
  98.4 0.1 reshape.133
  98.5 0.9 fusion.72
  99.5 46.5 %all-reduce.9.cloned.1.call-done = f32[8,2048]{1,0:T(8,128)} async-done(((f32[8,2048]{1,0:T(8,128)}), f32[8,2048]{1,0:T(8,128)}) %all-reduce.9.cloned.1.call-update) | async-done | bytes 65552 | tf_op jit(solution)/shard_map/psum | solution.py:52
  145.9 1.0 multiply_reduce_fusion.2
  146.9 5.4 %fusion.12 = f32[8,2048]{1,0:T(8,128)} fusion(bf16[2,1024,2048]{2,1,0:T(8,128)(2,1)} %param.19, bf16[2,2048,1024]{2,1,0:T(8,128)(2,1)} %param.18, f32[2048]{0:T(1024)S(1)} %bitcast.107, f32[8]{0:T(128)S(1)} %add_rsqrt_fusion.2, f32[8,2048]{1,0:T(8,128)} %all-reduce.9.cloned.1.call-done, bf16[8,2048]{1,0:T(8,128)(2,1)S(1)} %copy-done.1), kind=kOutput, calls=%fused_computation.16 | convolution fusion | flops 67264512 | bytes 8560672 | tf_op jit(solution)/shard_map/dot_general | solution.py:15
  152.4 45.1 %all-reduce.11.cloned.1.call-done = f32[8,2048]{1,0:T(8,128)} async-done(((f32[8,2048]{1,0:T(8,128)}), f32[8,2048]{1,0:T(8,128)}) %all-reduce.11.cloned.1.call-update) | async-done | bytes 65552 | tf_op jit(solution)/shard_map/psum | solution.py:54
  197.5 1.0 multiply_reduce_fusion.1
  198.4 0.1 multiply_convert_fusion.1
  198.5 2.0 fusion.67
  200.5 2.0 fusion.64
  202.5 4.6 %fusion.33 = bf16[8,2048]{1,0:T(8,128)(2,1)S(1)} fusion(bf16[8,2048]{1,0:T(8,128)(2,1)S(1)} %multiply_convert_fusion.1, bf16[2,2048,2048]{2,1,0:T(8,128)(2,1)} %param.14), kind=kOutput, calls=%fused_computation.41 | convolution fusion | flops 67125248 | bytes 8454144 | tf_op jit(solution)/shard_map/dot_general | solution.py:15
  207.1 0.1 broadcast_in_dim.107
  207.1 0.1 reshape.134
  207.3 3.0 fusion.147
  210.3 22.3 %pmax.15 = f32[8,8,4]{2,1,0:T(8,128)S(1)} all-reduce(f32[8,8,4]{2,1,0:T(8,128)S(1)} %get-tuple-element.25), channel_id=1, replica_groups=mesh['dp'=2,'sp'=8] {'sp'}, use_global_device_ids=true, to_apply=%region_11.12 | all-reduce | flops 256 | bytes 2048 | tf_op jit(solution)/shard_map/pmax | solution.py:48
  232.6 0.1 broadcast_in_dim.109
  232.7 0.4 fusion.78
  233.1 4.1 %fusion.55 = f32[8,8,4,64]{3,2,1,0:T(4,128)} fusion(pred[8,512]{1,0:T(8,128)(4,1)S(1)} %get-tuple-element.22, bf16[2,8,512,8,64]{2,4,3,1,0:T(8,128)(2,1)} %param.23, bf16[8,8,64]{2,1,0:T(8,128)(2,1)S(1)} %broadcast_in_dim.109, f32[8,8,4,512]{3,2,1,0:T(4,128)S(1)} %get-tuple-element.26, f32[8,8,4]{2,1,0:T(8,128)S(1)} %is-finite_select_fusion, ...), kind=kOutput, calls=%fused_computation.61 | convolution fusion | flops 19152896 | bytes 4798464 | tf_op jit(solution)/shard_map/bkgs,bskd->bkgd/dot_general | solution.py:47
  237.3 22.4 %psum.61 = f32[8,8,4]{2,1,0:T(8,128)S(1)} all-reduce(f32[8,8,4]{2,1,0:T(8,128)S(1)} %get-tuple-element.5), channel_id=1, replica_groups=mesh['dp'=2,'sp'=8] {'sp'}, use_global_device_ids=true, to_apply=%region_14.15 | all-reduce | flops 256 | bytes 2048 | tf_op jit(solution)/shard_map/psum | solution.py:49
  259.7 22.9 %all-reduce.13.cloned.1.call-done = f32[8,8,4,64]{3,2,1,0:T(4,128)} async-done(((f32[8,8,4,64]{3,2,1,0:T(4,128)}), f32[8,8,4,64]{3,2,1,0:T(4,128)}) %all-reduce.13.cloned.1.call-update) | async-done | bytes 65552 | tf_op jit(solution)/shard_map/psum | solution.py:49
  282.6 1.0 divide_convert_fusion
  283.7 0.1 reshape.136
  283.8 0.9 fusion.70
  284.7 0.2 all-reduce.17.cloned.1.call-start
  284.9 11.8 %broadcast_select_fusion.1 = (bf16[1,8,512,8,64]{2,4,3,1,0:T(8,128)(2,1)}, bf16[1,8,512,8,64]{2,4,3,1,0:T(8,128)(2,1)}, bf16[1,8,512,8,64]{2,4,3,1,0:T(8,128)(2,1)}, bf16[1,8,512,8,64]{2,4,3,1,0:T(8,128)(2,1)}) fusion(pred[8,512]{1,0:T(8,128)(4,1)S(1)} %get-tuple-element.22, bf16[2,8,512,8,64]{2,4,3,1,0:T(8,128)(2,1)} %param.23, ...), kind=kLoop, calls=%fused_computation.29 | loop fusion | flops 8388608 | bytes 33591296 | tf_op jit(solution)/shard_map/jit(_where)/select_n | solution.py:39
  296.6 34.4 %all-reduce.15.cloned.1.call-done = f32[8,2048]{1,0:T(8,128)} async-done(((f32[8,2048]{1,0:T(8,128)}), f32[8,2048]{1,0:T(8,128)}) %all-reduce.15.cloned.1.call-update) | async-done | bytes 65552 | tf_op jit(solution)/shard_map/psum | solution.py:52
  331.0 1.0 multiply_reduce_fusion
  332.0 5.3 %fusion.6 = f32[8,2048]{1,0:T(8,128)} fusion(bf16[2,1024,2048]{2,1,0:T(8,128)(2,1)} %param.19, bf16[2,2048,1024]{2,1,0:T(8,128)(2,1)} %param.18, f32[8,2048]{1,0:T(8,128)S(1)} %get-tuple-element.4, f32[2048]{0:T(1024)S(1)} %bitcast.106, f32[8]{0:T(128)S(1)} %add_rsqrt_fusion), kind=kOutput, calls=%fused_computation.8 | convolution fusion | flops 67231744 | bytes 8527904 | tf_op jit(solution)/shard_map/dot_general | solution.py:15
  337.4 11.6 %pad_maximum_fusion = (bf16[2,8,512,8,64]{2,4,3,1,0:T(8,128)(2,1)}, bf16[2,8,512,8,64]{2,4,3,1,0:T(8,128)(2,1)}) fusion(bf16[1,8,512,8,64]{2,4,3,1,0:T(8,128)(2,1)} %get-tuple-element.19, bf16[1,8,512,8,64]{2,4,3,1,0:T(8,128)(2,1)} %get-tuple-element.20, bf16[1,8,512,8,64]{2,4,3,1,0:T(8,128)(2,1)} %get-tuple-element.12, ...), kind=kLoop, calls=%fused_computation | loop fusion | flops 8388608 | bytes 33554432 | tf_op jit(solution)/shard_map/stack | solution.py:55
  348.9 33.6 %all-reduce.17.cloned.1.call-done = f32[8,2048]{1,0:T(8,128)} async-done(((f32[8,2048]{1,0:T(8,128)}), f32[8,2048]{1,0:T(8,128)}) %all-reduce.17.cloned.1.call-update) | async-done | bytes 65552 | tf_op jit(solution)/shard_map/psum | solution.py:54
  382.5 1.5 add_convert_fusion
  (33 shorter events, 0.5 us)
Async XLA Ops:
  7.2 90.2 %all-reduce.7.cloned.1.call-start = ((), (), s32[]{:S(2)}) async-start(), calls=%async_computation | async-start | bytes 262144 | tf_op jit(solution)/shard_map/psum | solution.py:49
  11.7 4.8 %copy-start.4 = (s32[8]{0:T(128)S(1)}, s32[8]{0:T(128)}, u32[]{:S(2)}) copy-start(s32[8]{0:T(128)} %param.13) | copy-start | bytes 100
  16.6 28.8 %copy-start.1 = (bf16[8,2048]{1,0:T(8,128)(2,1)S(1)}, bf16[8,2048]{1,0:T(8,128)(2,1)}, u32[]{:S(2)}) copy-start(bf16[8,2048]{1,0:T(8,128)(2,1)} %param.12) | copy-start | bytes 98308
  47.9 50.6 %copy-start = (bf16[2,256,2048]{2,1,0:T(8,128)(2,1)S(1)}, bf16[2,256,2048]{2,1,0:T(8,128)(2,1)}, u32[]{:S(2)}) copy-start(bf16[2,256,2048]{2,1,0:T(8,128)(2,1)} %param.17) | copy-start | bytes 6291460
  47.9 51.5 %copy-start.3 = (bf16[2,2048]{1,0:T(2,128)(2,1)S(1)}, bf16[2,2048]{1,0:T(2,128)(2,1)}, u32[]{:S(2)}) copy-start(bf16[2,2048]{1,0:T(2,128)(2,1)} %param.21) | copy-start | bytes 24580
  52.2 93.7 %all-reduce.9.cloned.1.call-start = ((), (), s32[]{:S(2)}) async-start(), calls=%async_computation.1 | async-start | bytes 131072 | tf_op jit(solution)/shard_map/psum | solution.py:52
  99.4 98.1 %all-reduce.11.cloned.1.call-start = ((), (), s32[]{:S(2)}) async-start(), calls=%async_computation.2 | async-start | bytes 131072 | tf_op jit(solution)/shard_map/psum | solution.py:54
  146.9 50.6 %copy-start.2 = (f32[8,2048]{1,0:T(8,128)S(1)}, f32[8,2048]{1,0:T(8,128)}, u32[]{:S(2)}) copy-start(f32[8,2048]{1,0:T(8,128)} %all-reduce.9.cloned.1.call-done) | copy-start | bytes 196612
  152.3 130.3 %all-reduce.13.cloned.1.call-start = ((), (), s32[]{:S(2)}) async-start(), calls=%async_computation.3 | async-start | bytes 262144 | tf_op jit(solution)/shard_map/psum | solution.py:49
  237.3 93.8 %all-reduce.15.cloned.1.call-start = ((), (), s32[]{:S(2)}) async-start(), calls=%async_computation.4 | async-start | bytes 131072 | tf_op jit(solution)/shard_map/psum | solution.py:52
  284.7 97.9 %all-reduce.17.cloned.1.call-start = ((), (), s32[]{:S(2)}) async-start(), calls=%async_computation.5 | async-start | bytes 131072 | tf_op jit(solution)/shard_map/psum | solution.py:54
Sparse Core Ops, SparseCore 0:
  52.3 44.9 all-reduce.6
  100.9 44.9 all-reduce.8
  152.5 44.9 all-reduce.10
  237.4 45.1 all-reduce.12
  286.1 44.9 all-reduce.14
  337.5 44.9 all-reduce.16
where the time goes:
time: 392 us; the launch traced here: 391 us
  waiting for transfers between devices  205 us (52%)
  blocking collectives  92.9 us (24%)
  matrix products  44.1 us (11%)
  other arithmetic  33.1 us (8%)
  between operations  14.3 us (4%)
    psum x2, waiting for transfers between devices, local(): h = h + lax.psum(_mm(att, wo[l]), 'sp')  80.8 us
    psum x2, waiting for transfers between devices, local(): h = h + lax.psum(_mm(u, w2[l]), 'sp')  78.6 us
    pmax x2, blocking collectives, local(): c = jnp.exp(m - lax.pmax(m, 'sp'))  48.1 us
    psum x2, waiting for transfers between devices, local(): o, den = lax.psum((o * c[..., None], den * c), 'sp')  45.6 us
    psum x2, blocking collectives, local(): o, den = lax.psum((o * c[..., None], den * c), 'sp')  44.7 us
    dot_general x10, matrix products, _mm(): return jnp.dot(a, w, preferred_element_type=jnp.float32)  29.7 us
    select_n x1, other arithmetic, local(): vl = jnp.where(write, v, vc[l])  11.8 us
    another operation x1, other arithmetic, local(): return (h.astype(jnp.bfloat16), jnp.stack(ks), jnp.stack(vs))  11.6 us
  transfers between devices with their start and end apart: 6, of which 6 were waited for; matrix products, arithmetic and copies ran while one was open for 6% of the time, Pallas kernels for 0%

commit v1 on v0

v1 whole, which is shorter than its diff:
```python
import functools
import math

import jax
import jax.numpy as jnp
from jax import lax
from jax.experimental import pallas as pl
from jax.experimental.pallas import tpu as pltpu
from jax.sharding import PartitionSpec as P

EPS = 1e-6
F32 = jnp.float32
BF16 = jnp.bfloat16
MESH = pl.DeviceIdType.MESH
HBM = pl.BlockSpec(memory_space=pl.ANY)
VMEM = pl.BlockSpec(memory_space=pltpu.VMEM)
SMEM = pl.BlockSpec(memory_space=pltpu.SMEM)
N = 8
CH = 256


def _rms(h, g):
    r = lax.rsqrt(jnp.mean(h * h, axis=-1, keepdims=True) + EPS)
    return (h * r * g.astype(F32)).astype(BF16)


def _iota(shape, dim):
    return lax.broadcasted_iota(jnp.int32, shape, dim)


def _attend(l, first, *refs):
    h_ref, lens, g1, wq, wk, wv, kc, vc = refs[:8]
    refs = refs[8:] if first else refs[10:]
    out, ko, vo, w, kb, vb, qs, ps, st, wsem, ksem, vsem, kosem, vosem = refs
    b, s = kb.shape[0], kb.shape[2]

    loads = [pltpu.make_async_copy(wk.at[l], w.at[0], wsem.at[0]),
             pltpu.make_async_copy(wv.at[l], w.at[1], wsem.at[1])]
    for i in range(4):
        loads.append(pltpu.make_async_copy(wq.at[l, :, pl.ds(512 * i, 512)], w.at[2 + i], wsem.at[2 + i]))
    kin = [pltpu.make_async_copy(kc.at[l, i], kb.at[i], ksem.at[i]) for i in range(b)]
    vin = [pltpu.make_async_copy(vc.at[l, i], vb.at[i], vsem.at[i]) for i in range(b)]
    kout = [pltpu.make_async_copy(kb.at[i], ko.at[l, i], kosem.at[i]) for i in range(b)]
    vout = [pltpu.make_async_copy(vb.at[i], vo.at[l, i], vosem.at[i]) for i in range(b)]
    for c in loads + kin + vin:
        c.start()

    xn = _rms(h_ref[...].astype(F32), g1[l:l + 1, :])
    proj = []
    for i in range(6):
        loads[i].wait()
        proj.append(jnp.dot(xn, w[i], preferred_element_type=F32).astype(BF16).astype(F32))
    knew, vnew = proj[0], proj[1]

    lane = _iota((8, 128), 1)
    for r in range(32):
        t = proj[2 + r // 8][:, (r // 2 % 4) * 128:(r // 2 % 4) * 128 + 128]
        half = r // 4 % 2
        if r % 2 != half:
            t = pltpu.roll(t, 64, 1)
        qs[r * 8:r * 8 + 8, :] = jnp.where(lane // 64 == half, t, 0.0)

    base = lax.axis_index('sp') * s

    def write(buf, new, i):
        pos = lens[i] - 1 - base

        @pl.when((pos >= 0) & (pos < s))
        def _():
            blk = pl.multiple_of(pos // 128 * 128, 128)
            col = jnp.broadcast_to(new[i:i + 1, :], (128, s)).T
            hit = _iota((s, 128), 1) == pos % 128
            old = buf[i, :, pl.ds(blk, 128)].astype(F32)
            buf[i, :, pl.ds(blk, 128)] = jnp.where(hit, col, old).astype(BF16)

    for i in range(b):
        kin[i].wait()
        write(kb, knew, i)
        kout[i].start()
    slane = _iota((32, 128), 1)
    for i in range(b):
        sc = []
        for kp in range(4):
            q = qs[pl.ds(kp * 64 + i, 8, stride=8), :].astype(BF16)
            sc.append(jnp.dot(q, kb[i, kp * 128:kp * 128 + 128, :], preferred_element_type=F32))
        sc = jnp.concatenate(sc, axis=0) * 0.125
        sc = jnp.where(_iota((32, s), 1) < lens[i] - base, sc, -jnp.inf)
        m = jnp.max(sc, axis=1, keepdims=True)
        p = jnp.exp(sc - jnp.where(m == -jnp.inf, 0.0, m))
        den = jnp.sum(p, axis=1, keepdims=True)
        ps[i] = p.astype(BF16)
        st[i] = jnp.where(slane % 64 < 32, m, den)

    for i in range(b):
        vin[i].wait()
        write(vb, vnew, i)
        vout[i].start()
    mine = _iota((8, 128), 0) // 4 == lane // 64
    for i in range(b):
        for grp in range(2):
            o = lax.dot_general(ps[i, grp * 16:grp * 16 + 16, :], vb[i, grp * 256:grp * 256 + 256, :],
                                (((1,), (1,)), ((), ())), preferred_element_type=F32)
            for half in range(2):
                kp = grp * 2 + half
                v = jnp.where(mine, o[half * 8:half * 8 + 8, half * 128:half * 128 + 128],
                              st[i, kp * 8:kp * 8 + 8, :])
                out[pl.ds(kp * 64 + i, 4, stride=8), :] = v[0:4]
                out[pl.ds(kp * 64 + 32 + i, 4, stride=8), :] = v[4:8]
    for c in kout + vout:
        c.wait()


def _finish(l, h_ref, att, g2, wo, w1, w2, out, wob, w1b, w2b, arecv, psend, rrecv, hb, xn,
            wsem, asem, asem2, rsem, rsem2, gsem, gsem2):
    me = lax.axis_index('sp')
    loads = [pltpu.make_async_copy(src.at[l], dst, wsem.at[i])
             for i, (src, dst) in enumerate(((wo, wob), (w1, w1b), (w2, w2b)))]
    barrier = pltpu.get_barrier_semaphore()
    peer = [lax.rem(me + i, N) for i in range(N)]
    for i in range(1, N):
        pl.semaphore_signal(barrier, inc=1, device_id={'sp': peer[i]}, device_id_type=MESH)
    for c in loads:
        c.start()
    pl.semaphore_wait(barrier, N - 1)

    sent = []

    def send(src, dst, s0, s1, i):
        c = pltpu.make_async_remote_copy(src, dst, s0, s1, device_id={'sp': peer[i]}, device_id_type=MESH)
        c.start()
        sent.append(c)
        return c

    parts = [send(att.at[pl.ds(pl.multiple_of(peer[i] * 32, 32), 32), :], arecv.at[i - 1],
                  asem.at[i - 1], asem2.at[i - 1], i) for i in range(1, N)]
    tiles = [att[pl.ds(pl.multiple_of(me * 32, 32), 32), :]]
    for i in range(1, N):
        parts[i - 1].wait_recv()
        tiles.append(arecv[i - 1])
    lane = _iota((32, 128), 1)
    low = lane % 64 < 32
    ms, ls = [], []
    for t in tiles:
        r = pltpu.roll(t, 64, 1)
        ms.append(jnp.where(low, r, pltpu.roll(r, 32, 1)))
        ls.append(jnp.where(low, pltpu.roll(r, 96, 1), r))
    top = functools.reduce(jnp.maximum, ms)
    num, den = jnp.zeros_like(top), jnp.zeros_like(top)
    for t, m, d in zip(tiles, ms, ls):
        c = jnp.exp(m - top)
        num, den = num + c * t, den + c * d
    o = num / den
    even = jnp.broadcast_to(lax.rem(me, 2) == 0, o.shape)
    o = jnp.where(even, o, pltpu.roll(o, 64, 1))
    other = pltpu.roll(o, 64, 1)
    first = _iota((8, 128), 1) < 64
    lhs = jnp.concatenate([jnp.where(first, o[t * 16:t * 16 + 8], other[t * 16 + 8:t * 16 + 16])
                           for t in range(2)], axis=1).astype(BF16)

    def summed(k, lhs, w, resid):
        hops = []
        for i in range(1, N):
            cols = pl.ds(pl.multiple_of(peer[i] * CH, CH), CH)
            psend[k, i - 1] = jnp.dot(lhs, w[:, cols], preferred_element_type=F32)
            hops.append(send(psend.at[k, i - 1], rrecv.at[k, i - 1], rsem.at[k, i - 1], rsem2.at[k, i - 1], i))
        cols = pl.ds(pl.multiple_of(me * CH, CH), CH)
        acc = jnp.dot(lhs, w[:, cols], preferred_element_type=F32)
        for i in range(1, N):
            hops[i - 1].wait_recv()
            acc = acc + rrecv[k, i - 1]
        hb[k, me] = resid() + acc
        hops = [send(hb.at[k, me], hb.at[k, me], gsem.at[k, i - 1], gsem2.at[k, i - 1], i) for i in range(1, N)]
        for c in hops:
            c.wait_recv()

    loads[0].wait()
    summed(0, lhs, wob, lambda: h_ref[:, pl.ds(pl.multiple_of(me * CH, CH), CH)].astype(F32))
    hs = [hb[0, c] for c in range(N)]
    ss = sum(jnp.sum(x * x, axis=1, keepdims=True) for x in hs)
    r = lax.rsqrt(ss / (N * CH) + EPS)
    for c in range(N):
        g = g2[l:l + 1, c * CH:(c + 1) * CH].astype(F32)
        xn[:, c * CH:(c + 1) * CH] = (hs[c] * r * g).astype(BF16)
    loads[1].wait()
    u = jax.nn.gelu(jnp.dot(xn[...], w1b[...], preferred_element_type=F32)).astype(BF16)
    loads[2].wait()
    summed(1, u, w2b, lambda: hb[0, me])
    for c in range(N):
        out[:, c * CH:(c + 1) * CH] = hb[1, c].astype(out.dtype)
    for c in sent:
        c.wait_send()


def solution(mesh):
    kspec = P(None, 'dp', 'sp', None, None)
    DMA = pltpu.SemaphoreType.DMA

    def attend(l, h, lens, g1, wq, wk, wv, kt, vt, bufs):
        nl, b, d, s = kt.shape
        cache = jax.ShapeDtypeStruct(kt.shape, kt.dtype)
        first = not bufs
        return pl.pallas_call(
            functools.partial(_attend, l, first),
            out_shape=(jax.ShapeDtypeStruct((256, 128), F32), cache, cache),
            in_specs=[VMEM, SMEM, VMEM] + [HBM] * (5 if first else 7),
            out_specs=(VMEM, HBM, HBM),
            input_output_aliases={} if first else {8: 1, 9: 2},
            scratch_shapes=[
                pltpu.VMEM((6, wq.shape[1], 512), BF16),
                pltpu.VMEM((b, d, s), BF16), pltpu.VMEM((b, d, s), BF16),
                pltpu.VMEM((256, 128), F32), pltpu.VMEM((b, 32, s), BF16), pltpu.VMEM((b, 32, 128), F32),
                DMA((6,)), DMA((b,)), DMA((b,)), DMA((b,)), DMA((b,))],
            compiler_params=pltpu.CompilerParams(vmem_limit_bytes=60 << 20),
            name=f'attend{l}',
        )(h, lens, g1, wq, wk, wv, kt, vt, *bufs)

    def finish(l, h, att, g2, wo, w1, w2, dtype):
        return pl.pallas_call(
            functools.partial(_finish, l),
            out_shape=jax.ShapeDtypeStruct(h.shape, dtype),
            in_specs=[VMEM, VMEM, VMEM, HBM, HBM, HBM],
            out_specs=VMEM,
            scratch_shapes=[
                pltpu.VMEM(wo.shape[1:], BF16), pltpu.VMEM(w1.shape[1:], BF16), pltpu.VMEM(w2.shape[1:], BF16),
                pltpu.VMEM((N - 1, 32, 128), F32),
                pltpu.VMEM((2, N - 1, 8, CH), F32), pltpu.VMEM((2, N - 1, 8, CH), F32),
                pltpu.VMEM((2, N, 8, CH), F32), pltpu.VMEM(h.shape, BF16),
                DMA((3,)), DMA((N - 1,)), DMA((N - 1,)),
                DMA((2, N - 1)), DMA((2, N - 1)), DMA((2, N - 1)), DMA((2, N - 1))],
            compiler_params=pltpu.CompilerParams(collective_id=l, has_side_effects=True, vmem_limit_bytes=60 << 20),
            name=f'finish{l}',
        )(h, att, g2, wo, w1, w2)

    def local(x, lens, wq, wk, wv, wo, w1, w2, g1, g2, kc, vc):
        nl, b, s, kvh, dh = kc.shape
        kt = kc.transpose(0, 1, 3, 4, 2).reshape(nl, b, kvh * dh, s)
        vt = vc.transpose(0, 1, 3, 4, 2).reshape(nl, b, kvh * dh, s)
        h, bufs = x, ()
        for l in range(nl):
            att, *bufs = attend(l, h, lens, g1, wq, wk, wv, kt, vt, bufs)
            h = finish(l, h, att, g2, wo, w1, w2, BF16 if l == nl - 1 else F32)
        back = [t.reshape(nl, b, kvh, dh, s).transpose(0, 1, 4, 2, 3) for t in bufs]
        return h, *back

    return jax.shard_map(
        local, mesh=mesh,
        in_specs=(P('dp', None), P('dp'), P(), P(), P(), P(None, 'sp', None), P(None, None, 'sp'),
                  P(None, 'sp', None), P(), P(), kspec, kspec),
        out_specs=(P('dp', None), kspec, kspec), check_vma=False)
```

time: 392 us -> 75.5 us (0.19)
  waiting for transfers between devices: 205 us -> 0 us
  blocking collectives: 92.9 us -> 0 us
  Pallas kernels: 0 us -> 73.1 us
  matrix products: 44.1 us -> 0 us
  other arithmetic: 33.1 us -> 0 us
  between operations: 14.3 us -> 0.66 us
    psum x6 -> x0, waiting for transfers between devices: 205 us -> none  [the longest x2 80.8 us: local(): h = h + lax.psum(_mm(att, wo[l]), 'sp')]
    pallas_call x0 -> x4, Pallas kernels: none -> 73.1 us  [the longest x2 48.4 us: finish(): pl.pallas_call(functools.partial(_finish, l), out_shape=jax.ShapeDtypeStr...]
    pmax x2 -> x0, blocking collectives: 48.1 us -> none  [local(): c = jnp.exp(m - lax.pmax(m, 'sp'))]
    psum x2 -> x0, blocking collectives: 44.7 us -> none  [local(): o, den = lax.psum((o * c[..., None], den * c), 'sp')]
    dot_general x14 -> x0, matrix products: 44.1 us -> none  [the longest x10 29.7 us: _mm(): return jnp.dot(a, w, preferred_element_type=jnp.float32)]
    select_n x3 -> x0, other arithmetic: 11.8 us -> none  [the longest x1 11.8 us: local(): vl = jnp.where(write, v, vc[l])]
    another operation x1 -> x0, other arithmetic: 11.6 us -> none  [local(): return (h.astype(jnp.bfloat16), jnp.stack(ks), jnp.stack(vs))]
    reduce_sum x6 -> x0, other arithmetic: 4.52 us -> none  [the longest x4 3.8 us: _rms(): r = lax.rsqrt(jnp.mean(h * h, axis=-1, keepdims=True) + EPS)]
  transfers between devices with their start and end apart: 6 -> 0, of which waited for: 6 -> 0; matrix products, arithmetic and copies ran while one was open for 6% -> 0% of each run, Pallas kernels for 0% -> 0%
where the time goes in v1:
time: 75.5 us; the launch traced here: 75.2 us
  Pallas kernels  73.1 us (97%)
  local copies, waits for them, and re-layouts  1.38 us (2%)
    pallas_call x2, Pallas kernels, finish(): pl.pallas_call(functools.partial(_finish, l), out_shape=jax.ShapeDtypeStr...  48.4 us
    pallas_call x2, Pallas kernels, attend(): pl.pallas_call(functools.partial(_attend, l, first), out_shape=(jax.Shape...  24.7 us

profile of v1, /device:TPU:0, one launch (start us, length us, event | category | flops | bytes accessed | tf_op | source)
XLA Modules:
  0.0 75.2 jit_solution(4146389496712370403)
XLA Ops:
  0.6 12.3 %attend0.1 = (f32[256,128]{1,0:T(8,128)}, bf16[2,8,512,512]{3,2,1,0:T(8,128)(2,1)}, bf16[2,8,512,512]{3,2,1,0:T(8,128)(2,1)}) custom-call(bf16[8,2048]{1,0:T(8,128)(2,1)} %h_ref.1, s32[8]{0:T(128)} %refs_1_.3, bf16[2,2048]{1,0:T(2,128)(2,1)} %refs_2_.3, bf16[2,2048,2048]{2,1,0:T(8,128)(2,1)} %refs_3_.3, bf16[2,2048,512]{2,1,0:T(8,128)(2,1)} %refs_4_.3, ...), custom_call_target="tpu_custom_call" | custom-call | tf_op jit(solution)/shard_map/attend0/pallas_call | solution.py:202
  13.0 25.4 %finish0.1.refs_0_.h_ref = f32[8,2048]{1,0:T(8,128)} custom-call(bf16[8,2048]{1,0:T(8,128)(2,1)} %h_ref.1, f32[256,128]{1,0:T(8,128)} %get-tuple-element.9.att, bf16[2,2048]{1,0:T(2,128)(2,1)} %g2.3, bf16[2,256,2048]{2,1,0:T(8,128)(2,1)} %wo.3, bf16[2,2048,1024]{2,1,0:T(8,128)(2,1)} %w1.3, bf16[2,1024,2048]{2,1,0:T(8,128)(2,1)} %w2.3), custom_call_target="tpu_custom_call" | custom-call | tf_op jit(solution)/shard_map/finish0/pallas_call | solution.py:218
  38.3 12.4 %attend1.1 = (f32[256,128]{1,0:T(8,128)}, bf16[2,8,512,512]{3,2,1,0:T(8,128)(2,1)}, bf16[2,8,512,512]{3,2,1,0:T(8,128)(2,1)}) custom-call(f32[8,2048]{1,0:T(8,128)} %finish0.1.refs_0_.h_ref, s32[8]{0:T(128)} %refs_1_.3, bf16[2,2048]{1,0:T(2,128)(2,1)} %refs_2_.3, bf16[2,2048,2048]{2,1,0:T(8,128)(2,1)} %refs_3_.3, ...), custom_call_target="tpu_custom_call", output_to_operand_aliasing={{1}: (8, {}), {2}: (9, {})} | custom-call | tf_op jit(solution)/shard_map/attend1/pallas_call | solution.py:202
  50.7 23.1 %finish1.1 = bf16[8,2048]{1,0:T(8,128)(2,1)} custom-call(f32[8,2048]{1,0:T(8,128)} %finish0.1.refs_0_.h_ref, f32[256,128]{1,0:T(8,128)} %get-tuple-element.12.att, bf16[2,2048]{1,0:T(2,128)(2,1)} %g2.3, bf16[2,256,2048]{2,1,0:T(8,128)(2,1)} %wo.3, bf16[2,2048,1024]{2,1,0:T(8,128)(2,1)} %w1.3, bf16[2,1024,2048]{2,1,0:T(8,128)(2,1)} %w2.3), custom_call_target="tpu_custom_call" | custom-call | tf_op jit(solution)/shard_map/finish1/pallas_call | solution.py:218
  73.8 1.4 %copy.20 = bf16[8,2048]{1,0:T(8,128)(2,1)} copy(bf16[8,2048]{1,0:T(8,128)(2,1)} %finish1.1) | data formatting | bytes 65536

commit v2 on v0

v2 whole, which is shorter than its diff:
```python
import functools

import jax
import jax.numpy as jnp
from jax import lax
from jax.experimental import pallas as pl
from jax.experimental.pallas import tpu as pltpu
from jax.sharding import PartitionSpec as P

EPS = 1e-6
F32 = jnp.float32
BF16 = jnp.bfloat16
MESH = pl.DeviceIdType.MESH
HBM = pl.BlockSpec(memory_space=pl.ANY)
VMEM = pl.BlockSpec(memory_space=pltpu.VMEM)
SMEM = pl.BlockSpec(memory_space=pltpu.SMEM)
DMA = pltpu.SemaphoreType.DMA
N = 8
HALF = 1024


def _in(space, *arrays):
    return [pltpu.with_memory_space_constraint(a, space) for a in arrays]


def _iota(shape, dim):
    return lax.broadcasted_iota(jnp.int32, shape, dim)


def _peer(me, k):
    y, x, c = me // 4, me // 2 % 2, me % 2
    return (y + k // 4) % 2 * 4 + (x + k // 2 % 2) % 2 * 2 + (c + k % 2) % 2


def _project(h, g, w, wait):
    r = lax.rsqrt(jnp.mean(h * h, axis=-1, keepdims=True) + EPS)
    xn = (h * r * g).astype(BF16)
    out = []
    for i in range(6):
        wait(i)
        out.append(jnp.dot(xn, w[i], preferred_element_type=F32).astype(BF16).astype(F32))
    return out


def _partials(proj, lens, base, kb, vb, kwait, vwait, qs, sn, ps, pn, st, out):
    knew, vnew = proj[0], proj[1]
    b, s = kb.shape[0], kb.shape[2]
    lane = _iota((8, 128), 1)
    for r in range(32):
        t = proj[2 + r // 8][:, (r // 2 % 4) * 128:(r // 2 % 4) * 128 + 128]
        half = r // 4 % 2
        if r % 2 != half:
            t = pltpu.roll(t, 64, 1)
        t = jnp.where(lane // 64 == half, t, 0.0)
        qs[r * 8:r * 8 + 8, :] = t
        d = jnp.sum(t * knew[:, r // 8 * 128:r // 8 * 128 + 128], axis=1, keepdims=True)
        sn[r * 8:r * 8 + 8, :] = jnp.broadcast_to(d, (8, 128))
    slane = _iota((32, 128), 1) % 64 < 32
    for i in range(b):
        kwait(i)
        pos = lens[i] - 1 - base
        rows = [pl.ds(kp * 64 + i, 8, stride=8) for kp in range(4)]
        sc = jnp.concatenate([
            jnp.dot(qs[rows[kp], :].astype(BF16), kb[i, kp * 128:kp * 128 + 128, :], preferred_element_type=F32)
            for kp in range(4)], axis=0) * 0.125
        sc = jnp.where(_iota((32, s), 1) < pos, sc, -jnp.inf)
        new = jnp.concatenate([sn[rows[kp], :] for kp in range(4)], axis=0)[:, 0:1] * 0.125
        here = jnp.broadcast_to((pos >= 0) & (pos < s), new.shape)
        new = jnp.where(here, new, -jnp.inf)
        m = jnp.maximum(jnp.max(sc, axis=1, keepdims=True), new)
        safe = jnp.where(m == -jnp.inf, 0.0, m)
        p, pnew = jnp.exp(sc - safe), jnp.exp(new - safe)
        den = jnp.sum(p, axis=1, keepdims=True) + pnew
        ps[i] = p.astype(BF16)
        pn[i] = jnp.broadcast_to(pnew.astype(BF16).astype(F32), (32, 128))
        st[i] = jnp.where(slane, m, den)
    mine = _iota((8, 128), 0) // 4 == lane // 64
    for i in range(b):
        vwait(i)
        for grp in range(2):
            o = lax.dot_general(ps[i, grp * 16:grp * 16 + 16, :], vb[i, grp * 256:grp * 256 + 256, :],
                                (((1,), (1,)), ((), ())), preferred_element_type=F32)
            for half in range(2):
                kp = grp * 2 + half
                t = o[half * 8:half * 8 + 8, half * 128:half * 128 + 128]
                t = t + pn[i, kp * 8:kp * 8 + 8, :] * vnew[i:i + 1, kp * 128:kp * 128 + 128]
                v = jnp.where(mine, t, st[i, kp * 8:kp * 8 + 8, :])
                out[pl.ds(kp * 64 + i, 4, stride=8), :] = v[0:4]
                out[pl.ds(kp * 64 + 32 + i, 4, stride=8), :] = v[4:8]


class _Group:
    SCRATCH = (
        pltpu.VMEM((N, 32, 128), F32),
        pltpu.VMEM((2, 2, 8, HALF), F32),
        pltpu.VMEM((2, 2, 8, HALF), F32),
        pltpu.VMEM((2, 8, HALF), F32),
        pltpu.VMEM((2, 4, 8, HALF), F32),
        pltpu.VMEM((2, 2, 8, HALF), F32),
        DMA((N,)), DMA((N,)), DMA((2, 6)), DMA((2, 6)))

    def __init__(self, refs):
        (self.arecv, self.part, self.prec, self.csum, self.chips, self.hb,
         self.asend, self.aland, self.ssend, self.sland) = refs
        self.me = lax.axis_index('sp')
        self.sent = []

    def signal(self):
        self.barrier = pltpu.get_barrier_semaphore()
        for k in range(1, N):
            pl.semaphore_signal(self.barrier, inc=1, device_id={'sp': _peer(self.me, k)}, device_id_type=MESH)

    def enter(self):
        pl.semaphore_wait(self.barrier, N - 1)

    def send(self, src, dst, s0, s1, k):
        c = pltpu.make_async_remote_copy(src, dst, s0, s1, device_id={'sp': _peer(self.me, k)}, device_id_type=MESH)
        c.start()
        self.sent.append(c)
        return c

    def scatter(self, att):
        self.att = att
        self.parts = [
            self.send(att.at[pl.ds(pl.multiple_of(_peer(self.me, k) * 32, 32), 32), :], self.arecv.at[k],
                      self.asend.at[k], self.aland.at[k], k) for k in (7, 6, 5, 3, 4, 2, 1)]

    def combine(self):
        tiles = [self.att[pl.ds(pl.multiple_of(self.me * 32, 32), 32), :]]
        for c in self.parts:
            c.wait_recv()
        tiles += [self.arecv[k] for k in range(1, N)]
        low = _iota((32, 128), 1) % 64 < 32
        ms, ls = [], []
        for t in tiles:
            r = pltpu.roll(t, 64, 1)
            ms.append(jnp.where(low, r, pltpu.roll(r, 32, 1)))
            ls.append(jnp.where(low, pltpu.roll(r, 96, 1), r))
        top = functools.reduce(jnp.maximum, ms)
        num, den = jnp.zeros_like(top), jnp.zeros_like(top)
        for t, m, d in zip(tiles, ms, ls):
            c = jnp.exp(m - top)
            num, den = num + c * t, den + c * d
        o = num / den
        even = jnp.broadcast_to(self.me % 2 == 0, o.shape)
        o = jnp.where(even, o, pltpu.roll(o, 64, 1))
        other = pltpu.roll(o, 64, 1)
        first = _iota((8, 128), 1) < 64
        return jnp.concatenate([jnp.where(first, o[t * 16:t * 16 + 8], other[t * 16 + 8:t * 16 + 16])
                                for t in range(2)], axis=1).astype(BF16)

    def add(self, n, lhs, w, resid):
        me = self.me
        core, chip = me % 2, me // 2
        other = 1 - core

        def product(half):
            self.part[n, half] = jnp.dot(lhs, w[:, pl.ds(pl.multiple_of(half * HALF, HALF), HALF)],
                                         preferred_element_type=F32)

        def swap(half, i):
            return self.send(self.part.at[n, half], self.prec.at[n, half],
                             self.ssend.at[n, i], self.sland.at[n, i], 1)

        product(other)
        c0 = swap(other, 0)
        product(core)
        c1 = swap(core, 1)
        c0.wait_recv()
        self.csum[n] = self.part[n, core] + self.prec[n, core]
        hops = [self.send(self.csum.at[n], self.chips.at[n, chip], self.ssend.at[n, 1 + k // 2],
                          self.sland.at[n, 1 + k // 2], k) for k in (7, 5, 3)]
        c1.wait_recv()
        self.chips[n, chip] = self.part[n, other] + self.prec[n, other]
        for c in hops:
            c.wait_recv()
        t = self.chips
        self.hb[n, other] = resid(other) + ((t[n, 0] + t[n, 1]) + (t[n, 2] + t[n, 3]))
        c = self.send(self.hb.at[n, other], self.hb.at[n, other], self.ssend.at[n, 5], self.sland.at[n, 5], 1)
        c.wait_recv()

    def layer(self, h, g2, wo, w1, w2, xn, wait):
        lhs = self.combine()
        wait(0)
        self.add(0, lhs, wo, lambda half: h[:, pl.ds(pl.multiple_of(half * HALF, HALF), HALF)].astype(F32))
        hs = [self.hb[0, 0], self.hb[0, 1]]
        ss = sum(jnp.sum(x * x, axis=1, keepdims=True) for x in hs)
        r = lax.rsqrt(ss / (2 * HALF) + EPS)
        for c in range(2):
            xn[:, c * HALF:(c + 1) * HALF] = (hs[c] * r * g2[:, c * HALF:(c + 1) * HALF].astype(F32)).astype(BF16)
        wait(1)
        u = jax.nn.gelu(jnp.dot(xn[...], w1[...], preferred_element_type=F32)).astype(BF16)
        wait(2)
        self.add(1, u, w2, lambda half: self.hb[0, half])

    def leave(self):
        for c in self.sent:
            c.wait_send()


def _copies(pairs, sem):
    return [pltpu.make_async_copy(src, dst, sem.at[i]) for i, (src, dst) in enumerate(pairs)]


def _qkv_weights(l, wq, wk, wv, w, sem):
    return _copies([(wk.at[l], w.at[0]), (wv.at[l], w.at[1])]
                   + [(wq.at[l, :, pl.ds(512 * i, 512)], w.at[2 + i]) for i in range(4)], sem)


def _first(x, lens, g1, g2, wq, wk, wv, wo, w1, w2, kc, vc,
           h, new, kb0, vb0, kb1, vb1, wn,
           w, wob, w1b, w2b, qs, sn, ps, pn, st, att, xn, wsem, nsem, ksem, vsem, osem, csem, *group):
    grp = _Group(group)
    grp.signal()
    b, s = kb0.shape[0], kb0.shape[2]
    qkv = _qkv_weights(0, wq, wk, wv, w, wsem)
    kin = _copies([(kc.at[0, i], kb0.at[i]) for i in range(b)], ksem)
    vin = _copies([(vc.at[0, i], vb0.at[i]) for i in range(b)], vsem)
    rest = _copies([(wo.at[0], wob), (w1.at[0], w1b), (w2.at[0], w2b)], osem)
    for c in qkv + kin + vin + rest:
        c.start()
    proj = _project(x[...].astype(F32), g1[0:1, :].astype(F32), w, lambda i: qkv[i].wait())
    new[0], new[1] = proj[0], proj[1]
    _partials(proj, lens, grp.me * s, kb0, vb0, lambda i: kin[i].wait(), lambda i: vin[i].wait(),
              qs, sn, ps, pn, st, att)
    grp.enter()
    grp.scatter(att)
    ahead = _qkv_weights(1, wq, wk, wv, wn, nsem) + _copies([(kc.at[1], kb1), (vc.at[1], vb1)], csem)
    for c in ahead:
        c.start()
    grp.layer(x, g2[0:1, :], wob, w1b, w2b, xn, lambda i: rest[i].wait())
    for c in range(2):
        h[:, c * HALF:(c + 1) * HALF] = grp.hb[1, c]
    for c in ahead:
        c.wait()
    grp.leave()


def _second(h, lens, g1, new, kb0, vb0, kb1, vb1, w,
            att, ko, vo, qs, sn, ps, pn, st, cols, blocks, bsem, csem):
    b, s = kb0.shape[0], kb0.shape[2]
    base = lax.axis_index('sp') * s
    caches = [(kb0, ko, 0), (vb0, vo, 0), (kb1, ko, 1), (vb1, vo, 1)]
    bulk = [pltpu.make_async_copy(src.at[i], dst.at[l, i], bsem.at[n, i])
            for n, (src, dst, l) in enumerate(caches) for i in range(b)]
    for c in bulk:
        c.start()
    proj = _project(h[...], g1[1:2, :].astype(F32), w, lambda i: None)
    _partials(proj, lens, base, kb1, vb1, lambda i: None, lambda i: None, qs, sn, ps, pn, st, att)
    for n, x in enumerate((new[0], new[1], proj[0], proj[1])):
        cols[n] = jnp.broadcast_to(x[:, None, :], (b, 16, s)).reshape(b * 16, s).T

    def each(n, i, do):
        src, dst, l = caches[n]
        pos = lens[i] - 1 - base

        @pl.when((pos >= 0) & (pos < s))
        def _():
            at = pl.ds(pl.multiple_of(pos // 128 * 128, 128), 128)
            do(src, pos, at, pltpu.make_async_copy(blocks.at[n, i], dst.at[l, i, :, at], csem.at[n, i]),
               bulk[n * b + i])

        return (pos >= 0) & (pos < s)

    def fill(n, i):
        def do(src, pos, at, c, whole):
            hit = _iota((s, 128), 1) == pos % 128
            col = cols[n, :, i * 16:i * 16 + 1]
            blocks[n, i] = jnp.where(hit, col, src[i, :, at].astype(F32)).astype(BF16)
            whole.wait()
            c.start()

        here = each(n, i, do)

        @pl.when(jnp.logical_not(here))
        def _():
            bulk[n * b + i].wait()

    for n in range(4):
        for i in range(b):
            fill(n, i)
    for n in range(4):
        for i in range(b):
            each(n, i, lambda src, pos, at, c, whole: c.wait())


def _third(h, att, g2, wo, w1, w2, y, wob, w1b, w2b, xn, osem, *group):
    grp = _Group(group)
    grp.signal()
    rest = _copies([(wo.at[1], wob), (w1.at[1], w1b), (w2.at[1], w2b)], osem)
    for c in rest:
        c.start()
    grp.enter()
    grp.scatter(att)
    grp.layer(h, g2[1:2, :], wob, w1b, w2b, xn, lambda i: rest[i].wait())
    for c in range(2):
        y[:, c * HALF:(c + 1) * HALF] = grp.hb[1, c].astype(y.dtype)
    grp.leave()


def solution(mesh):
    kspec = P(None, 'dp', 'sp', None, None)

    def local(x, lens, wq, wk, wv, wo, w1, w2, g1, g2, kc, vc):
        nl, b, s, kvh, dh = kc.shape
        d = kvh * dh
        kt = kc.transpose(0, 1, 3, 4, 2).reshape(nl, b, d, s)
        vt = vc.transpose(0, 1, 3, 4, 2).reshape(nl, b, d, s)
        slice_, weights = pltpu.VMEM((b, d, s), BF16), pltpu.VMEM((6, wq.shape[1], d), BF16)
        mlp = [pltpu.VMEM(w.shape[1:], BF16) for w in (wo, w1, w2)]
        local_ = [pltpu.VMEM((256, 128), F32), pltpu.VMEM((256, 128), F32), pltpu.VMEM((b, 32, s), BF16),
                  pltpu.VMEM((b, 32, 128), F32), pltpu.VMEM((b, 32, 128), F32)]
        partial = pltpu.VMEM((256, 128), F32)
        rows = pltpu.VMEM(x.shape, BF16)

        def call(body, name, n_in, out_shape, out_specs, scratch, collective_id=None, limit=64):
            return pl.pallas_call(
                body, out_shape=out_shape, in_specs=n_in, out_specs=out_specs, scratch_shapes=scratch,
                compiler_params=pltpu.CompilerParams(
                    collective_id=collective_id, has_side_effects=collective_id is not None,
                    vmem_limit_bytes=limit << 20), name=name)

        h, new, *held = call(
            _first, 'first', [VMEM, SMEM, VMEM, VMEM] + [HBM] * 8,
            (pltpu.VMEM(x.shape, F32), pltpu.VMEM((2, b, d), F32), slice_, slice_, slice_, slice_, weights),
            (VMEM,) * 7,
            [weights, *mlp, *local_, partial, rows,
             DMA((6,)), DMA((6,)), DMA((b,)), DMA((b,)), DMA((3,)), DMA((2,)), *_Group.SCRATCH], 0, limit=28,
        )(x, lens, g1, g2, *_in(pltpu.HBM, wq, wk, wv, wo, w1, w2, kt, vt))
        cache = jax.ShapeDtypeStruct(kt.shape, kt.dtype)
        att, ko, vo = call(
            _second, 'second', [VMEM, SMEM, VMEM] + [VMEM] * 6, (pltpu.VMEM((256, 128), F32), cache, cache),
            (VMEM, HBM, HBM),
            [*local_, pltpu.VMEM((4, s, 128), F32), pltpu.VMEM((4, b, d, 128), BF16), DMA((4, b)), DMA((4, b))], limit=14,
        )(h, lens, g1, *_in(pltpu.VMEM, new, *held))
        y = call(
            _third, 'third', [VMEM, VMEM, VMEM] + [HBM] * 3, jax.ShapeDtypeStruct(x.shape, BF16), VMEM,
            [*mlp, rows, DMA((3,)), *_Group.SCRATCH], 1, limit=16,
        )(h, att, g2, *_in(pltpu.HBM, wo, w1, w2))
        back = [t.reshape(nl, b, kvh, dh, s).transpose(0, 1, 4, 2, 3) for t in (ko, vo)]
        return y, *back

    return jax.shard_map(
        local, mesh=mesh,
        in_specs=(P('dp', None), P('dp'), P(), P(), P(), P(None, 'sp', None), P(None, None, 'sp'),
                  P(None, 'sp', None), P(), P(), kspec, kspec),
        out_specs=(P('dp', None), kspec, kspec), check_vma=False)
```

time: 392 us -> 63.4 us (0.16)
  waiting for transfers between devices: 205 us -> 0 us
  blocking collectives: 92.9 us -> 0 us
  Pallas kernels: 0 us -> 61.9 us
  matrix products: 44.1 us -> 0 us
  other arithmetic: 33.1 us -> 0 us
  between operations: 14.3 us -> 0.7 us
    psum x6 -> x0, waiting for transfers between devices: 205 us -> none  [the longest x2 80.8 us: local(): h = h + lax.psum(_mm(att, wo[l]), 'sp')]
    pallas_call x0 -> x3, Pallas kernels: none -> 61.9 us  [the longest x1 34.3 us: local(): call(_first, 'first', [VMEM, SMEM, VMEM, VMEM] + [HBM] * 8, (pltpu.VMEM(x...]
    pmax x2 -> x0, blocking collectives: 48.1 us -> none  [local(): c = jnp.exp(m - lax.pmax(m, 'sp'))]
    psum x2 -> x0, blocking collectives: 44.7 us -> none  [local(): o, den = lax.psum((o * c[..., None], den * c), 'sp')]
    dot_general x14 -> x0, matrix products: 44.1 us -> none  [the longest x10 29.7 us: _mm(): return jnp.dot(a, w, preferred_element_type=jnp.float32)]
    select_n x3 -> x0, other arithmetic: 11.8 us -> none  [the longest x1 11.8 us: local(): vl = jnp.where(write, v, vc[l])]
    another operation x1 -> x0, other arithmetic: 11.6 us -> none  [local(): return (h.astype(jnp.bfloat16), jnp.stack(ks), jnp.stack(vs))]
    reduce_sum x6 -> x0, other arithmetic: 4.52 us -> none  [the longest x4 3.8 us: _rms(): r = lax.rsqrt(jnp.mean(h * h, axis=-1, keepdims=True) + EPS)]
  transfers between devices with their start and end apart: 6 -> 0, of which waited for: 6 -> 0; matrix products, arithmetic and copies ran while one was open for 6% -> 0% of each run, Pallas kernels for 0% -> 0%
where the time goes in v2:
time: 63.4 us; the launch traced here: 63.2 us
  Pallas kernels  61.9 us (98%)
  between operations  0.7 us (1%)
    pallas_call x1, Pallas kernels, local(): call(_first, 'first', [VMEM, SMEM, VMEM, VMEM] + [HBM] * 8, (pltpu.VMEM(x...  34.3 us
    pallas_call x1, Pallas kernels, local(): call(_third, 'third', [VMEM, VMEM, VMEM] + [HBM] * 3, jax.ShapeDtypeStruc...  17.4 us
    pallas_call x1, Pallas kernels, local(): call(_second, 'second', [VMEM, SMEM, VMEM] + [VMEM] * 6, (pltpu.VMEM((256...  10.2 us

profile of v2, /device:TPU:0, one launch (start us, length us, event | category | flops | bytes accessed | tf_op | source)
XLA Modules:
  0.0 63.2 jit_solution(8296351538897376866)
XLA Ops:
  0.6 0.0 copy-start.1
  0.6 0.0 copy-start.2
  0.7 34.3 %first.1 = (f32[8,2048]{1,0:T(8,128)S(1)}, f32[2,8,512]{2,1,0:T(8,128)S(1)}, bf16[8,512,512]{2,1,0:T(8,128)(2,1)S(1)}, bf16[8,512,512]{2,1,0:T(8,128)(2,1)S(1)},...) custom-call(bf16[8,2048]{1,0:T(8,128)(2,1)} %x.1, s32[8]{0:T(128)} %lens.3, ...), custom_call_target="tpu_custom_call" | custom-call | tf_op jit(solution)/shard_map/first/pallas_call | solution.py:323
  34.9 0.0 copy-done.1
  34.9 0.0 copy-done.2
  35.0 0.0 copy-start
  35.0 10.2 %second.1 = (f32[256,128]{1,0:T(8,128)S(1)}, bf16[2,8,512,512]{3,2,1,0:T(8,128)(2,1)}, bf16[2,8,512,512]{3,2,1,0:T(8,128)(2,1)}) custom-call(f32[8,2048]{1,0:T(8,128)S(1)} %get-tuple-element.13.h, s32[8]{0:T(128)S(1)} %copy-done.2, bf16[2,2048]{1,0:T(2,128)(2,1)S(1)} %copy-done.1, f32[2,8,512]{2,1,0:T(8,128)S(1)} %get-tuple-element.14.new, ...), custom_call_target="tpu_custom_call" | custom-call | tf_op jit(solution)/shard_map/second/pallas_call | solution.py:331
  45.2 0.0 copy-done
  45.2 17.4 %third.1 = bf16[8,2048]{1,0:T(8,128)(2,1)S(1)} custom-call(f32[8,2048]{1,0:T(8,128)S(1)} %get-tuple-element.13.h, f32[256,128]{1,0:T(8,128)S(1)} %get-tuple-element.20.att, bf16[2,2048]{1,0:T(2,128)(2,1)S(1)} %copy-done, bf16[2,256,2048]{2,1,0:T(8,128)(2,1)} %wo.3, bf16[2,2048,1024]{2,1,0:T(8,128)(2,1)} %w1.3, bf16[2,1024,2048]{2,1,0:T(8,128)(2,1)} %w2.3), custom_call_target="tpu_custom_call" | custom-call | tf_op jit(solution)/shard_map/third/pallas_call | solution.py:336
  62.6 0.6 copy.16
Async XLA Ops:
  0.6 34.3 %copy-start.1 = (bf16[2,2048]{1,0:T(2,128)(2,1)S(1)}, bf16[2,2048]{1,0:T(2,128)(2,1)}, u32[]{:S(2)}) copy-start(bf16[2,2048]{1,0:T(2,128)(2,1)} %g1.3) | copy-start | bytes 24580
  0.6 34.3 %copy-start.2 = (s32[8]{0:T(128)S(1)}, s32[8]{0:T(128)}, u32[]{:S(2)}) copy-start(s32[8]{0:T(128)} %lens.3) | copy-start | bytes 100
  35.0 10.2 %copy-start = (bf16[2,2048]{1,0:T(2,128)(2,1)S(1)}, bf16[2,2048]{1,0:T(2,128)(2,1)}, u32[]{:S(2)}) copy-start(bf16[2,2048]{1,0:T(2,128)(2,1)} %g2.3) | copy-start | bytes 24580

commit v3 on v2

--- a/solution.py
+++ b/solution.py
@@ -36,7 +36,7 @@
     r = lax.rsqrt(jnp.mean(h * h, axis=-1, keepdims=True) + EPS)
     xn = (h * r * g).astype(BF16)
     out = []
-    for i in range(6):
+    for i in range(w.shape[0]):
         wait(i)
         out.append(jnp.dot(xn, w[i], preferred_element_type=F32).astype(BF16).astype(F32))
     return out
@@ -56,8 +56,8 @@
         d = jnp.sum(t * knew[:, r // 8 * 128:r // 8 * 128 + 128], axis=1, keepdims=True)
         sn[r * 8:r * 8 + 8, :] = jnp.broadcast_to(d, (8, 128))
     slane = _iota((32, 128), 1) % 64 < 32
-    for i in range(b):
-        kwait(i)
+    kwait()
+    for i in range(b):
         pos = lens[i] - 1 - base
         rows = [pl.ds(kp * 64 + i, 8, stride=8) for kp in range(4)]
         sc = jnp.concatenate([
@@ -75,8 +75,8 @@
         pn[i] = jnp.broadcast_to(pnew.astype(BF16).astype(F32), (32, 128))
         st[i] = jnp.where(slane, m, den)
     mine = _iota((8, 128), 0) // 4 == lane // 64
-    for i in range(b):
-        vwait(i)
+    vwait()
+    for i in range(b):
         for grp in range(2):
             o = lax.dot_general(ps[i, grp * 16:grp * 16 + 16, :], vb[i, grp * 256:grp * 256 + 256, :],
                                 (((1,), (1,)), ((), ())), preferred_element_type=F32)
@@ -202,31 +202,76 @@
     return [pltpu.make_async_copy(src, dst, sem.at[i]) for i, (src, dst) in enumerate(pairs)]
 
 
+def _start(copies):
+    for c in copies:
+        c.start()
+
+
+def _wait(copies):
+    for c in copies:
+        c.wait()
+
+
 def _qkv_weights(l, wq, wk, wv, w, sem):
     return _copies([(wk.at[l], w.at[0]), (wv.at[l], w.at[1])]
                    + [(wq.at[l, :, pl.ds(512 * i, 512)], w.at[2 + i]) for i in range(4)], sem)
 
 
-def _first(x, lens, g1, g2, wq, wk, wv, wo, w1, w2, kc, vc,
+def _first(x_, lens_, g1_, g2_, wq, wk, wv, wo, w1, w2, kc, vc,
            h, new, kb0, vb0, kb1, vb1, wn,
-           w, wob, w1b, w2b, qs, sn, ps, pn, st, att, xn, wsem, nsem, ksem, vsem, osem, csem, *group):
+           w, wob, w1b, w2b, qs, sn, ps, pn, st, att, xn, wsem, nsem, ksem, vsem, osem, csem,
+           x, lens, g1, g2, msem, pr, psem, *group):
+    small = _copies([(x_, x), (g1_, g1), (lens_, lens), (g2_, g2)], msem)
+    for c in small:
+        c.start()
     grp = _Group(group)
     grp.signal()
     b, s = kb0.shape[0], kb0.shape[2]
-    qkv = _qkv_weights(0, wq, wk, wv, w, wsem)
+    core = grp.me % 2
+    rows = w.shape[1]
+
+    def pieces(src, i, n, start):
+        return [pltpu.make_async_copy(src.at[pl.ds(j * rows // n, rows // n), :],
+                                      w.at[i, pl.ds(j * rows // n, rows // n), :], wsem.at[start + j])
+                for j in range(n)]
+
+    @pl.when(core == 0)
+    def _():
+        _start(pieces(wk.at[0], 0, 8, 0))
+
+    @pl.when(core == 1)
+    def _():
+        _start(pieces(wv.at[0], 0, 8, 0))
+
+    quarter = [wq.at[0, :, pl.ds(pl.multiple_of(core * 1024 + 512 * i, 512), 512)] for i in range(2)]
+    qkv = [pieces(wk.at[0], 0, 8, 0), pieces(quarter[0], 1, 4, 8), pieces(quarter[1], 2, 4, 12)]
     kin = _copies([(kc.at[0, i], kb0.at[i]) for i in range(b)], ksem)
-    vin = _copies([(vc.at[0, i], vb0.at[i]) for i in range(b)], vsem)
+    vin = _copies([(vc.at[0, pl.ds(2 * i, 2)], vb0.at[pl.ds(2 * i, 2)]) for i in range(b // 2)], vsem)
     rest = _copies([(wo.at[0], wob), (w1.at[0], w1b), (w2.at[0], w2b)], osem)
-    for c in qkv + kin + vin + rest:
-        c.start()
-    proj = _project(x[...].astype(F32), g1[0:1, :].astype(F32), w, lambda i: qkv[i].wait())
+    _start(qkv[1] + qkv[2])
+    _wait(small)
+    grp.enter()
+
+    def arrived(i):
+        _wait(qkv[i])
+        if i == 1:
+            _start(kin)
+        if i == 2:
+            _start(vin)
+
+    mine = _project(x[...].astype(F32), g1[0:1, :].astype(F32), w, arrived)
+    for i in range(3):
+        pr[core, i] = mine[i].astype(BF16)
+    c = grp.send(pr.at[core], pr.at[core], psem.at[0], psem.at[1], 1)
+    c.wait_recv()
+    proj = [pr[0, 0], pr[1, 0], pr[0, 1], pr[0, 2], pr[1, 1], pr[1, 2]]
+    proj = [t.astype(F32) for t in proj]
     new[0], new[1] = proj[0], proj[1]
-    _partials(proj, lens, grp.me * s, kb0, vb0, lambda i: kin[i].wait(), lambda i: vin[i].wait(),
+    _partials(proj, lens, grp.me * s, kb0, vb0, lambda: _wait(kin), lambda: _wait(vin),
               qs, sn, ps, pn, st, att)
-    grp.enter()
     grp.scatter(att)
     ahead = _qkv_weights(1, wq, wk, wv, wn, nsem) + _copies([(kc.at[1], kb1), (vc.at[1], vb1)], csem)
-    for c in ahead:
+    for c in rest + ahead:
         c.start()
     grp.layer(x, g2[0:1, :], wob, w1b, w2b, xn, lambda i: rest[i].wait())
     for c in range(2):
@@ -243,45 +288,39 @@
     caches = [(kb0, ko, 0), (vb0, vo, 0), (kb1, ko, 1), (vb1, vo, 1)]
     bulk = [pltpu.make_async_copy(src.at[i], dst.at[l, i], bsem.at[n, i])
             for n, (src, dst, l) in enumerate(caches) for i in range(b)]
-    for c in bulk:
-        c.start()
+
+    @pl.loop(0, b)
+    def _(i):
+        for n, (src, dst, l) in enumerate(caches):
+            pltpu.make_async_copy(src.at[i], dst.at[l, i], bsem.at[n, i]).start()
+
     proj = _project(h[...], g1[1:2, :].astype(F32), w, lambda i: None)
-    _partials(proj, lens, base, kb1, vb1, lambda i: None, lambda i: None, qs, sn, ps, pn, st, att)
+    _partials(proj, lens, base, kb1, vb1, lambda: None, lambda: None, qs, sn, ps, pn, st, att)
     for n, x in enumerate((new[0], new[1], proj[0], proj[1])):
         cols[n] = jnp.broadcast_to(x[:, None, :], (b, 16, s)).reshape(b * 16, s).T
 
-    def each(n, i, do):
-        src, dst, l = caches[n]
+    def owned(i, do):
         pos = lens[i] - 1 - base
 
         @pl.when((pos >= 0) & (pos < s))
         def _():
             at = pl.ds(pl.multiple_of(pos // 128 * 128, 128), 128)
-            do(src, pos, at, pltpu.make_async_copy(blocks.at[n, i], dst.at[l, i, :, at], csem.at[n, i]),
-               bulk[n * b + i])
-
-        return (pos >= 0) & (pos < s)
-
-    def fill(n, i):
-        def do(src, pos, at, c, whole):
+            for n, (src, dst, l) in enumerate(caches):
+                do(n, src, pos, at, pltpu.make_async_copy(blocks.at[n, i], dst.at[l, i, :, at], csem.at[n, i]))
+
+    def fill(i):
+        def do(n, src, pos, at, c):
             hit = _iota((s, 128), 1) == pos % 128
-            col = cols[n, :, i * 16:i * 16 + 1]
-            blocks[n, i] = jnp.where(hit, col, src[i, :, at].astype(F32)).astype(BF16)
-            whole.wait()
-            c.start()
-
-        here = each(n, i, do)
-
-        @pl.when(jnp.logical_not(here))
-        def _():
-            bulk[n * b + i].wait()
-
-    for n in range(4):
-        for i in range(b):
-            fill(n, i)
-    for n in range(4):
-        for i in range(b):
-            each(n, i, lambda src, pos, at, c, whole: c.wait())
+            blocks[n, i] = jnp.where(hit, cols[n, :, i * 16:i * 16 + 1], src[i, :, at].astype(F32)).astype(BF16)
+        owned(i, do)
+
+    for i in range(b):
+        fill(i)
+    _wait(bulk)
+    for i in range(b):
+        owned(i, lambda n, src, pos, at, c: c.start())
+    for i in range(b):
+        owned(i, lambda n, src, pos, at, c: c.wait())
 
 
 def _third(h, att, g2, wo, w1, w2, y, wob, w1b, w2b, xn, osem, *group):
@@ -321,12 +360,15 @@
                     vmem_limit_bytes=limit << 20), name=name)
 
         h, new, *held = call(
-            _first, 'first', [VMEM, SMEM, VMEM, VMEM] + [HBM] * 8,
+            _first, 'first', [HBM] * 12,
             (pltpu.VMEM(x.shape, F32), pltpu.VMEM((2, b, d), F32), slice_, slice_, slice_, slice_, weights),
             (VMEM,) * 7,
-            [weights, *mlp, *local_, partial, rows,
-             DMA((6,)), DMA((6,)), DMA((b,)), DMA((b,)), DMA((3,)), DMA((2,)), *_Group.SCRATCH], 0, limit=28,
-        )(x, lens, g1, g2, *_in(pltpu.HBM, wq, wk, wv, wo, w1, w2, kt, vt))
+            [pltpu.VMEM((3, wq.shape[1], d), BF16), *mlp, *local_, partial, rows,
+             DMA((16,)), DMA((6,)), DMA((b,)), DMA((b,)), DMA((3,)), DMA((2,)),
+             rows, pltpu.SMEM(lens.shape, lens.dtype), pltpu.VMEM(g1.shape, BF16), pltpu.VMEM(g2.shape, BF16), DMA((4,)),
+             pltpu.VMEM((2, 3, b, d), BF16), DMA((2,)),
+             *_Group.SCRATCH], 0, limit=22,
+        )(*_in(pltpu.HBM, x, lens, g1, g2, wq, wk, wv, wo, w1, w2, kt, vt))
         cache = jax.ShapeDtypeStruct(kt.shape, kt.dtype)
         att, ko, vo = call(
             _second, 'second', [VMEM, SMEM, VMEM] + [VMEM] * 6, (pltpu.VMEM((256, 128), F32), cache, cache),

time: 63.4 us -> 52.8 us (0.83)
  Pallas kernels: 61.9 us -> 51.4 us
    pallas_call x1, Pallas kernels: 34.3 us -> 26.1 us  [local(): call(_first, 'first', [HBM] * 12, (pltpu.VMEM(x.shape, F32), pltpu.VMEM((...]
    pallas_call x1, Pallas kernels: 10.2 us -> 6.92 us  [local(): call(_second, 'second', [VMEM, SMEM, VMEM] + [VMEM] * 6, (pltpu.VMEM((256...]
    pallas_call x1, Pallas kernels: 17.4 us -> 18.3 us  [local(): call(_third, 'third', [VMEM, VMEM, VMEM] + [HBM] * 3, jax.ShapeDtypeStruc...]
where the time goes in v3:
time: 52.8 us; the launch traced here: 52.7 us
  Pallas kernels  51.4 us (97%)
  between operations  0.7 us (1%)
  local copies, waits for them, and re-layouts  0.63 us (1%)
    pallas_call x1, Pallas kernels, local(): call(_first, 'first', [HBM] * 12, (pltpu.VMEM(x.shape, F32), pltpu.VMEM((...  26.1 us
    pallas_call x1, Pallas kernels, local(): call(_third, 'third', [VMEM, VMEM, VMEM] + [HBM] * 3, jax.ShapeDtypeStruc...  18.3 us
    pallas_call x1, Pallas kernels, local(): call(_second, 'second', [VMEM, SMEM, VMEM] + [VMEM] * 6, (pltpu.VMEM((256...  6.92 us

profile of v3, /device:TPU:0, one launch (start us, length us, event | category | flops | bytes accessed | tf_op | source)
XLA Modules:
  0.0 52.7 jit_solution(17219390465199102530)
XLA Ops:
  0.6 0.0 copy-start.1
  0.6 0.0 copy-start.2
  0.7 26.1 %first.1 = (f32[8,2048]{1,0:T(8,128)S(1)}, f32[2,8,512]{2,1,0:T(8,128)S(1)}, bf16[8,512,512]{2,1,0:T(8,128)(2,1)S(1)}, bf16[8,512,512]{2,1,0:T(8,128)(2,1)S(1)},...) custom-call(bf16[8,2048]{1,0:T(8,128)(2,1)} %x_.1, s32[8]{0:T(128)} %lens.1, ...), custom_call_target="tpu_custom_call" | custom-call | tf_op jit(solution)/shard_map/first/pallas_call | solution.py:362
  26.8 0.0 copy-done.1
  26.8 0.0 copy-done.2
  26.8 0.0 copy-start
  26.8 6.9 %second.1 = (f32[256,128]{1,0:T(8,128)S(1)}, bf16[2,8,512,512]{3,2,1,0:T(8,128)(2,1)}, bf16[2,8,512,512]{3,2,1,0:T(8,128)(2,1)}) custom-call(f32[8,2048]{1,0:T(8,128)S(1)} %get-tuple-element.13.h, s32[8]{0:T(128)S(1)} %copy-done.2, bf16[2,2048]{1,0:T(2,128)(2,1)S(1)} %copy-done.1, f32[2,8,512]{2,1,0:T(8,128)S(1)} %get-tuple-element.14.new, ...), custom_call_target="tpu_custom_call" | custom-call | tf_op jit(solution)/shard_map/second/pallas_call | solution.py:373
  33.8 0.0 copy-done
  33.8 18.3 %third.1 = bf16[8,2048]{1,0:T(8,128)(2,1)S(1)} custom-call(f32[8,2048]{1,0:T(8,128)S(1)} %get-tuple-element.13.h, f32[256,128]{1,0:T(8,128)S(1)} %get-tuple-element.20.att, bf16[2,2048]{1,0:T(2,128)(2,1)S(1)} %copy-done, bf16[2,256,2048]{2,1,0:T(8,128)(2,1)} %wo.3, bf16[2,2048,1024]{2,1,0:T(8,128)(2,1)} %w1.3, bf16[2,1024,2048]{2,1,0:T(8,128)(2,1)} %w2.3), custom_call_target="tpu_custom_call" | custom-call | tf_op jit(solution)/shard_map/third/pallas_call | solution.py:378
  52.1 0.6 %copy.16 = bf16[8,2048]{1,0:T(8,128)(2,1)} copy(bf16[8,2048]{1,0:T(8,128)(2,1)S(1)} %third.1) | data formatting | bytes 65536
Async XLA Ops:
  0.6 26.2 %copy-start.1 = (bf16[2,2048]{1,0:T(2,128)(2,1)S(1)}, bf16[2,2048]{1,0:T(2,128)(2,1)}, u32[]{:S(2)}) copy-start(bf16[2,2048]{1,0:T(2,128)(2,1)} %g1.1) | copy-start | bytes 24580
  0.6 26.2 %copy-start.2 = (s32[8]{0:T(128)S(1)}, s32[8]{0:T(128)}, u32[]{:S(2)}) copy-start(s32[8]{0:T(128)} %lens.1) | copy-start | bytes 100
  26.8 6.9 %copy-start = (bf16[2,2048]{1,0:T(2,128)(2,1)S(1)}, bf16[2,2048]{1,0:T(2,128)(2,1)}, u32[]{:S(2)}) copy-start(bf16[2,2048]{1,0:T(2,128)(2,1)} %g2.1) | copy-start | bytes 24580

commit v4 on v3

--- a/solution.py
+++ b/solution.py
@@ -154,18 +154,20 @@
         core, chip = me % 2, me // 2
         other = 1 - core
 
-        def product(half):
+        def swap(i):
+            half = (other + i) % 2
+            return pltpu.make_async_remote_copy(
+                self.part.at[n, half], self.prec.at[n, half], self.ssend.at[n, i], self.sland.at[n, i],
+                device_id={'sp': _peer(me, 1)}, device_id_type=MESH)
+
+        for i in range(2):
+            half = (other + i) % 2
             self.part[n, half] = jnp.dot(lhs, w[:, pl.ds(pl.multiple_of(half * HALF, HALF), HALF)],
                                          preferred_element_type=F32)
-
-        def swap(half, i):
-            return self.send(self.part.at[n, half], self.prec.at[n, half],
-                             self.ssend.at[n, i], self.sland.at[n, i], 1)
-
-        product(other)
-        c0 = swap(other, 0)
-        product(core)
-        c1 = swap(core, 1)
+            swap(i).start()
+
+        c0, c1 = swap(0), swap(1)
+        self.sent += [c0, c1]
         c0.wait_recv()
         self.csum[n] = self.part[n, core] + self.prec[n, core]
         hops = [self.send(self.csum.at[n], self.chips.at[n, chip], self.ssend.at[n, 1 + k // 2],
@@ -281,46 +283,45 @@
     grp.leave()
 
 
-def _second(h, lens, g1, new, kb0, vb0, kb1, vb1, w,
-            att, ko, vo, qs, sn, ps, pn, st, cols, blocks, bsem, csem):
+def _second(h, lens, g1, new, kb0_, vb0_, kb1_, vb1_, w,
+            att, ko, vo, kb0, vb0, kb1, vb1, qs, sn, ps, pn, st, bsem):
     b, s = kb0.shape[0], kb0.shape[2]
     base = lax.axis_index('sp') * s
     caches = [(kb0, ko, 0), (vb0, vo, 0), (kb1, ko, 1), (vb1, vo, 1)]
-    bulk = [pltpu.make_async_copy(src.at[i], dst.at[l, i], bsem.at[n, i])
-            for n, (src, dst, l) in enumerate(caches) for i in range(b)]
+
+    def bulk(n, i):
+        src, dst, l = caches[n]
+        return pltpu.make_async_copy(src.at[i], dst.at[l, i], bsem.at[n, i])
+
+    def here(i):
+        pos = lens[i] - 1 - base
+        return (pos >= 0) & (pos < s)
 
     @pl.loop(0, b)
     def _(i):
-        for n, (src, dst, l) in enumerate(caches):
-            pltpu.make_async_copy(src.at[i], dst.at[l, i], bsem.at[n, i]).start()
-
+        @pl.when(jnp.logical_not(here(i)))
+        def _():
+            for n in range(4):
+                bulk(n, i).start()
+
+    def write(ns, news):
+        for i in range(b):
+            @pl.when(here(i))
+            def _():
+                pos = lens[i] - 1 - base
+                at = pl.ds(pl.multiple_of(pos // 128 * 128, 128), 128)
+                hit = _iota((s, 128), 1) == pos % 128
+                for n, x in zip(ns, news):
+                    col = jnp.broadcast_to(x[i:i + 1, :], (128, s)).T
+                    buf = caches[n][0]
+                    buf[i, :, at] = jnp.where(hit, col, buf[i, :, at].astype(F32)).astype(BF16)
+                    bulk(n, i).start()
+
+    write((0, 1), (new[0], new[1]))
     proj = _project(h[...], g1[1:2, :].astype(F32), w, lambda i: None)
+    write((2, 3), proj[:2])
     _partials(proj, lens, base, kb1, vb1, lambda: None, lambda: None, qs, sn, ps, pn, st, att)
-    for n, x in enumerate((new[0], new[1], proj[0], proj[1])):
-        cols[n] = jnp.broadcast_to(x[:, None, :], (b, 16, s)).reshape(b * 16, s).T
-
-    def owned(i, do):
-        pos = lens[i] - 1 - base
-
-        @pl.when((pos >= 0) & (pos < s))
-        def _():
-            at = pl.ds(pl.multiple_of(pos // 128 * 128, 128), 128)
-            for n, (src, dst, l) in enumerate(caches):
-                do(n, src, pos, at, pltpu.make_async_copy(blocks.at[n, i], dst.at[l, i, :, at], csem.at[n, i]))
-
-    def fill(i):
-        def do(n, src, pos, at, c):
-            hit = _iota((s, 128), 1) == pos % 128
-            blocks[n, i] = jnp.where(hit, cols[n, :, i * 16:i * 16 + 1], src[i, :, at].astype(F32)).astype(BF16)
-        owned(i, do)
-
-    for i in range(b):
-        fill(i)
-    _wait(bulk)
-    for i in range(b):
-        owned(i, lambda n, src, pos, at, c: c.start())
-    for i in range(b):
-        owned(i, lambda n, src, pos, at, c: c.wait())
+    _wait([bulk(n, i) for n in range(4) for i in range(b)])
 
 
 def _third(h, att, g2, wo, w1, w2, y, wob, w1b, w2b, xn, osem, *group):
@@ -352,9 +353,10 @@
         partial = pltpu.VMEM((256, 128), F32)
         rows = pltpu.VMEM(x.shape, BF16)
 
-        def call(body, name, n_in, out_shape, out_specs, scratch, collective_id=None, limit=64):
+        def call(body, name, n_in, out_shape, out_specs, scratch, collective_id=None, limit=64, aliases={}):
             return pl.pallas_call(
                 body, out_shape=out_shape, in_specs=n_in, out_specs=out_specs, scratch_shapes=scratch,
+                input_output_aliases=aliases,
                 compiler_params=pltpu.CompilerParams(
                     collective_id=collective_id, has_side_effects=collective_id is not None,
                     vmem_limit_bytes=limit << 20), name=name)
@@ -370,10 +372,10 @@
              *_Group.SCRATCH], 0, limit=22,
         )(*_in(pltpu.HBM, x, lens, g1, g2, wq, wk, wv, wo, w1, w2, kt, vt))
         cache = jax.ShapeDtypeStruct(kt.shape, kt.dtype)
-        att, ko, vo = call(
-            _second, 'second', [VMEM, SMEM, VMEM] + [VMEM] * 6, (pltpu.VMEM((256, 128), F32), cache, cache),
-            (VMEM, HBM, HBM),
-            [*local_, pltpu.VMEM((4, s, 128), F32), pltpu.VMEM((4, b, d, 128), BF16), DMA((4, b)), DMA((4, b))], limit=14,
+        att, ko, vo, *_ = call(
+            _second, 'second', [VMEM, SMEM, VMEM] + [VMEM] * 6,
+            (pltpu.VMEM((256, 128), F32), cache, cache) + (slice_,) * 4, (VMEM, HBM, HBM) + (VMEM,) * 4,
+            [*local_, DMA((4, b))], limit=8, aliases={4: 3, 5: 4, 6: 5, 7: 6},
         )(h, lens, g1, *_in(pltpu.VMEM, new, *held))
         y = call(
             _third, 'third', [VMEM, VMEM, VMEM] + [HBM] * 3, jax.ShapeDtypeStruct(x.shape, BF16), VMEM,

time: 52.8 us -> 51.8 us (0.981)
  Pallas kernels: 51.4 us -> 50.3 us
    pallas_call x1, Pallas kernels: 18.3 us -> 17.5 us  [local(): call(_third, 'third', [VMEM, VMEM, VMEM] + [HBM] * 3, jax.ShapeDtypeStruc...]
where the time goes in v4:
time: 51.8 us; the launch traced here: 51.6 us
  Pallas kernels  50.3 us (97%)
  between operations  0.7 us (1%)
  local copies, waits for them, and re-layouts  0.63 us (1%)
    pallas_call x1, Pallas kernels, local(): call(_first, 'first', [HBM] * 12, (pltpu.VMEM(x.shape, F32), pltpu.VMEM((...  26.1 us
    pallas_call x1, Pallas kernels, local(): call(_third, 'third', [VMEM, VMEM, VMEM] + [HBM] * 3, jax.ShapeDtypeStruc...  17.5 us
    pallas_call x1, Pallas kernels, local(): call(_second, 'second', [VMEM, SMEM, VMEM] + [VMEM] * 6, (pltpu.VMEM((256...  6.64 us

profile of v4, /device:TPU:0, one launch (start us, length us, event | category | flops | bytes accessed | tf_op | source)
XLA Modules:
  0.0 51.6 jit_solution(3003939880524849478)
XLA Ops:
  0.6 0.0 copy-start.1
  0.6 0.0 copy-start.2
  0.7 26.1 %first.1 = (f32[8,2048]{1,0:T(8,128)S(1)}, f32[2,8,512]{2,1,0:T(8,128)S(1)}, bf16[8,512,512]{2,1,0:T(8,128)(2,1)S(1)}, bf16[8,512,512]{2,1,0:T(8,128)(2,1)S(1)},...) custom-call(bf16[8,2048]{1,0:T(8,128)(2,1)} %x_.1, s32[8]{0:T(128)} %lens.1, ...), custom_call_target="tpu_custom_call" | custom-call | tf_op jit(solution)/shard_map/first/pallas_call | solution.py:364
  26.8 0.0 copy-done.1
  26.8 0.0 copy-done.2
  26.8 0.0 copy-start
  26.8 6.6 %second.1 = (f32[256,128]{1,0:T(8,128)S(1)}, bf16[2,8,512,512]{3,2,1,0:T(8,128)(2,1)}, bf16[2,8,512,512]{3,2,1,0:T(8,128)(2,1)}, bf16[8,512,512]{2,1,0:T(8,128)(...) custom-call(f32[8,2048]{1,0:T(8,128)S(1)} %get-tuple-element.13.h, ...), custom_call_target="tpu_custom_call", output_to_operand_aliasing={{3}: (4, {}), {4}: (5, {}), {5}: (6, {}), {6}: (7, {})} | custom-call | tf_op jit(solution)/shard_map/second/pallas_call | solution.py:375
  33.5 0.0 copy-done
  33.5 17.5 %third.1 = bf16[8,2048]{1,0:T(8,128)(2,1)S(1)} custom-call(f32[8,2048]{1,0:T(8,128)S(1)} %get-tuple-element.13.h, f32[256,128]{1,0:T(8,128)S(1)} %get-tuple-element.20.att, bf16[2,2048]{1,0:T(2,128)(2,1)S(1)} %copy-done, bf16[2,256,2048]{2,1,0:T(8,128)(2,1)} %wo.3, bf16[2,2048,1024]{2,1,0:T(8,128)(2,1)} %w1.3, bf16[2,1024,2048]{2,1,0:T(8,128)(2,1)} %w2.3), custom_call_target="tpu_custom_call" | custom-call | tf_op jit(solution)/shard_map/third/pallas_call | solution.py:380
  51.0 0.6 %copy.24 = bf16[8,2048]{1,0:T(8,128)(2,1)} copy(bf16[8,2048]{1,0:T(8,128)(2,1)S(1)} %third.1) | data formatting | bytes 65536
Async XLA Ops:
  0.6 26.2 %copy-start.1 = (bf16[2,2048]{1,0:T(2,128)(2,1)S(1)}, bf16[2,2048]{1,0:T(2,128)(2,1)}, u32[]{:S(2)}) copy-start(bf16[2,2048]{1,0:T(2,128)(2,1)} %g1.1) | copy-start | bytes 24580
  0.6 26.2 %copy-start.2 = (s32[8]{0:T(128)S(1)}, s32[8]{0:T(128)}, u32[]{:S(2)}) copy-start(s32[8]{0:T(128)} %lens.1) | copy-start | bytes 100
  26.8 6.7 %copy-start = (bf16[2,2048]{1,0:T(2,128)(2,1)S(1)}, bf16[2,2048]{1,0:T(2,128)(2,1)}, u32[]{:S(2)}) copy-start(bf16[2,2048]{1,0:T(2,128)(2,1)} %g2.1) | copy-start | bytes 24580
